TPU v7x, 32 devices: a whole 2x2x4 slice. The times are simulated.
32 devices in a mesh: member: 2 (over y), lat: 4 (over z), lon: 2 (over x), lev: 2 (over core).
Axes of the slice: x: 2, y: 2, z: 4, core: 2. Of those that a mesh axis runs over, the one named last changes fastest.
Arguments:
- perturbation: bfloat16 [4, 64, 16, 8, 128], P('member', 'lev', 'lat', 'lon'), parts along dimension 0, may hold values from -6 to 6
- adjoint_forcing: bfloat16 [4, 64, 16, 8, 128], P('member', 'lev', 'lat', 'lon'), parts along dimension 0, may hold values from -6 to 6
- source_rows: int32 [16, 8, 4], P('lat', 'lon'), may hold values from 0 to 15, as said below
- source_cols: int32 [16, 8, 4], P('lat', 'lon'), may hold values from 0 to 7, as said below
- cubic_weights: bfloat16 [16, 8, 4, 128, 128], P('lat', 'lon'), may hold values from -1.5 to 1.5
Outputs:
- tangent_out: bfloat16 [4, 64, 16, 8, 128], P('member', 'lev', 'lat', 'lon'), parts along dimension 0
- adjoint_out: bfloat16 [4, 64, 16, 8, 128], P('member', 'lev', 'lat', 'lon'), parts along dimension 0
There are 2 independent parts, one for each index of `member`. A program takes and returns all parts, laid end to end along the dimension named above; an argument that names none is the same for every part. Nothing has to cross between parts.
Inputs may be any that keep to these rules, and one draw needn't show every extreme that they name: source_rows[i, j, k] differs from i by at most 8. source_cols[i, j, k] is j + d modulo 8 with d from -1 to 1, and from -2 to 2 where i lies in the first or last 4 block rows.
All inputs are finite; a program needn't handle non-finite values.
Results may differ from a plain program's by a relative error of at most 0.004.
Values may be sent and summed in bfloat16 or wider, within the bound.
A program may use at most 64 MiB of HBM per device.

v0:
```python
import functools
import jax
import jax.numpy as jnp
from jax import lax
from jax.experimental import pallas as pl
from jax.experimental.pallas import tpu as pltpu
from jax.sharding import PartitionSpec as P

POLAR_ROWS = 4
REACH = 2
HALO = 2
BANDS = 2 * REACH + 1
MESH = pl.DeviceIdType.MESH


def exchange(
    sizes,
    where_ref, own_ref, forcing_ref, onehot_ref, weights_hbm,
    tangent_ref, adjoint_ref,
    ext, weights, contrib, spread, x_out, x_in, lent, far_out, far_in, near_out, near_in,
    weight_sem, own_sem, fwd_send, fwd_recv, lend_send, lend_recv, z_send, z_recv, x_send, x_recv, ax_send, ax_recv, az_send, az_recv,
):
    lat_count, lon_count, rows, cols, stencil = sizes
    depth, cells = own_ref.shape[1], own_ref.shape[2]
    span = cols + 2 * HALO
    tile = rows * cols
    targets = tile
    picks = targets * stencil
    places = BANDS * span * rows
    half = cols // 2
    z = lax.axis_index("lat")
    x = lax.axis_index("lon")
    west = lax.rem(x + lon_count - 1, lon_count)
    east = lax.rem(x + 1, lon_count)
    polar = (z * rows < POLAR_ROWS) | ((z + 1) * rows > lat_count * rows - POLAR_ROWS)
    sides = ({"lon": west}, {"lon": east})
    steps = (1, -1)

    def there(offset):
        return (z + offset >= 0) & (z + offset < lat_count)

    def place(band, column):
        return ((band + REACH) * span + column) * rows

    barrier = pltpu.get_barrier_semaphore()
    for side in sides:
        pl.semaphore_signal(barrier, inc=1, device_id=side, device_id_type=MESH)
    for step in steps:
        @pl.when(there(step))
        def _():
            pl.semaphore_signal(barrier, inc=1, device_id={"lat": z + step}, device_id_type=MESH)

    weight_copy = pltpu.make_async_copy(weights_hbm, weights, weight_sem)
    weight_copy.start()
    own_copy = pltpu.make_async_copy(
        own_ref, ext.at[pl.ds(place(0, HALO), tile)], own_sem
    )
    own_copy.start()
    peers = len(sides) + (2 if lat_count > 2 else lat_count - 1)
    inner = there(1) & there(-1)

    @pl.when(inner)
    def _():
        pl.semaphore_wait(barrier, peers)

    @pl.when(jnp.logical_not(inner))
    def _():
        pl.semaphore_wait(barrier, peers - 1 if lat_count > 2 else peers)

    def z_copy(d, hop, part):
        source_band = -steps[d] if hop else 0
        band = -steps[d] * (hop + 1)
        offset = part * half
        size = half * rows
        if hop:
            src = ext.at[pl.ds(place(source_band, HALO + offset), size)]
        else:
            src = own_ref.at[pl.ds(offset * rows, size)]
        return pltpu.make_async_remote_copy(
            src_ref=src,
            dst_ref=ext.at[pl.ds(place(band, HALO + offset), size)],
            send_sem=z_send.at[d, hop, part],
            recv_sem=z_recv.at[d, hop, part],
            device_id={"lat": z + steps[d]},
            device_id_type=MESH,
        )

    def x_copy(band, side, j):
        mine = j if side == 0 else cols - 1 - j
        lands = cols + HALO + j if side == 0 else HALO - 1 - j
        if band == 0:
            src = own_ref.at[pl.ds(mine * rows, rows)]
        else:
            src = ext.at[pl.ds(place(band, HALO + mine), rows)]
        return pltpu.make_async_remote_copy(
            src_ref=src,
            dst_ref=ext.at[pl.ds(place(band, lands), rows)],
            send_sem=x_send.at[band + REACH, side, j],
            recv_sem=x_recv.at[band + REACH, side, j],
            device_id=sides[side],
            device_id_type=MESH,
        )

    def ax_copy(band, side, j):
        return pltpu.make_async_remote_copy(
            src_ref=x_out.at[band + REACH, side, j],
            dst_ref=x_in.at[band + REACH, side, j],
            send_sem=ax_send.at[band + REACH, side, j],
            recv_sem=ax_recv.at[band + REACH, side, j],
            device_id=sides[side],
            device_id_type=MESH,
        )

    def az_copy(d, near, part):
        return pltpu.make_async_remote_copy(
            src_ref=(near_out if near else far_out).at[d, part],
            dst_ref=(near_in if near else far_in).at[d, part],
            send_sem=az_send.at[d, near, part],
            recv_sem=az_recv.at[d, near, part],
            device_id={"lat": z + steps[d]},
            device_id_type=MESH,
        )

    lending = lat_count >= 4
    poles = ((0, 1), (lat_count - 1, -1)) if lending else ()

    def fwd_copy(pole, step, i, side):
        column = HALO + cols if side == 0 else HALO - 1
        return pltpu.make_async_remote_copy(
            src_ref=ext.at[pl.ds(place(i * step, column), rows)],
            dst_ref=ext.at[pl.ds(place((i + 1) * step, column), rows)],
            send_sem=fwd_send.at[i, side],
            recv_sem=fwd_recv.at[i, side],
            device_id={"lat": pole},
            device_id_type=MESH,
        )

    def lend_copy(pole, step, i, side):
        return pltpu.make_async_remote_copy(
            src_ref=x_out.at[(i + 1) * step + REACH, side, 0],
            dst_ref=lent.at[i, side],
            send_sem=lend_send.at[i, side],
            recv_sem=lend_recv.at[i, side],
            device_id={"lat": pole + step},
            device_id_type=MESH,
        )

    def x_all(make, band, act, which=(0, 1)):
        @pl.when(there(band))
        def _():
            def edge():
                for side in range(2):
                    act(make(band, side, 0), band, side, 0)

            if 0 in which:
                if band != 0 and lending:
                    pl.when(jnp.logical_not(polar))(edge)
                else:
                    edge()
            if 1 in which:
                @pl.when(polar)
                def _():
                    for side in range(2):
                        act(make(band, side, 1), band, side, 1)

    def start(copy, *_):
        copy.start()

    def wait_send(copy, *_):
        copy.wait_send()

    def wait_recv(copy, *_):
        copy.wait_recv()

    for d in range(2):
        @pl.when(there(steps[d]))
        def _():
            for part in range(2):
                z_copy(d, 0, part).start()
    x_all(x_copy, 0, start)

    weight_copy.wait()

    def contribute(t, carry):
        block = weights[pl.ds(t * stencil, stencil)].reshape(stencil * cells, cells)
        part = lax.dot_general(
            forcing_ref[t], block, (((1,), (1,)), ((), ())), preferred_element_type=jnp.float32
        )
        for k in range(stencil):
            first = pl.multiple_of((t * stencil + k) * depth, depth)
            contrib[pl.ds(first, depth), :] = part[:, k * cells : (k + 1) * cells]
        return carry

    lax.fori_loop(0, targets, contribute, 0, unroll=2)

    def spread_rows(pair, carry):
        pieces = []
        for i in range(2):
            value = contrib[pl.ds(pair * 2 + i, picks, stride=depth), :]
            high = value.astype(jnp.bfloat16)
            low = (value - high.astype(jnp.float32)).astype(jnp.bfloat16)
            pieces.append(jnp.concatenate([high, low], axis=0))
        summed = jnp.dot(
            onehot_ref[...],
            jnp.concatenate(pieces, axis=1),
            preferred_element_type=jnp.float32,
        )
        for i in range(2):
            spread[pl.ds(pair * 2 + i, places, stride=depth), :] = summed[
                :, i * cells : (i + 1) * cells
            ]
        return carry

    lax.fori_loop(0, depth // 2, spread_rows, 0, unroll=2)

    def at(first, count):
        return pl.ds(first * depth, count * depth)

    def away(side, j):
        return HALO - 1 - j if side == 0 else HALO + cols + j

    def ax_start(copy, band, side, j):
        value = spread[at(place(band, away(side, j)), rows), :].astype(jnp.bfloat16)
        x_out[band + REACH, side, j] = value.reshape(rows, depth, cells)
        copy.start()

    def ax_finish(copy, band, side, j):
        copy.wait_recv()
        column = HALO + cols - 1 - j if side == 0 else HALO + j
        here = at(place(band, column), rows)
        value = x_in[band + REACH, side, j].astype(jnp.float32)
        spread[here, :] += value.reshape(rows * depth, cells)

    for pole, step in poles:
        @pl.when(z == pole)
        def _():
            for i in (1, 0):
                for side in range(2):
                    ax_start(lend_copy(pole, step, i, side), (i + 1) * step, side, 0)
    for band in (2, -2):
        x_all(ax_copy, band, ax_start)
    for d in range(2):
        @pl.when(there(-steps[d]))
        def _():
            for part in range(2):
                z_copy(d, 0, part).wait_recv()

                @pl.when(there(steps[d]))
                def _():
                    z_copy(d, 1, part).start()
        x_all(x_copy, -steps[d], start)

    borrows = {step: z == pole + step for pole, step in poles}
    for step in steps:
        if lending:
            @pl.when(jnp.logical_not(borrows[step]))
            def _():
                x_all(ax_copy, step, ax_start)
        else:
            x_all(ax_copy, step, ax_start)
    x_all(x_copy, 0, wait_recv, (0,))
    for pole, step in poles:
        @pl.when(z == pole + step)
        def _():
            for side in range(2):
                fwd_copy(pole, step, 0, side).start()

    for d in range(2):
        x_all(ax_copy, 2 * steps[d], ax_finish)

        @pl.when(there(2 * steps[d]))
        def _():
            for part in range(cols):
                here = at(place(2 * steps[d], HALO + part), rows)
                value = spread[here, :].astype(jnp.bfloat16)
                far_out[d, part] = value.reshape(rows, depth, cells)
                az_copy(d, 0, part).start()

    def borrow(pole, step, i):
        for side in range(2):
            lend_copy(pole, step, i, side).wait_recv()
            here = at(place(i * step, away(side, 0)), rows)
            value = lent[i, side].astype(jnp.float32)
            spread[here, :] += value.reshape(rows * depth, cells)

    for pole, step in poles:
        @pl.when(z == pole + step)
        def _():
            borrow(pole, step, 1)
            x_all(ax_copy, step, ax_start)
            borrow(pole, step, 0)
    x_all(ax_copy, 0, ax_start)

    for d in range(2):
        @pl.when(there(-2 * steps[d]))
        def _():
            for part in range(2):
                z_copy(d, 1, part).wait_recv()
        x_all(x_copy, -2 * steps[d], start)
    for band in (1, -1):
        x_all(x_copy, band, wait_recv, (0,))
    for pole, step in poles:
        @pl.when(z == pole + step)
        def _():
            for side in range(2):
                fwd_copy(pole, step, 1, side).start()

    for d in range(2):
        x_all(ax_copy, steps[d], ax_finish)

        @pl.when(there(steps[d]))
        def _():
            for part in range(cols):
                here = at(place(steps[d], HALO + part), rows)

                @pl.when(there(-steps[d]))
                def _():
                    az_copy(d, 0, part).wait_recv()
                    value = far_in[d, part].astype(jnp.float32)
                    spread[here, :] += value.reshape(rows * depth, cells)

                value = spread[here, :].astype(jnp.bfloat16)
                near_out[d, part] = value.reshape(rows, depth, cells)
                az_copy(d, 1, part).start()

    own_copy.wait()
    for band in range(-REACH, REACH + 1):
        x_all(x_copy, band, wait_recv, (0, 1) if abs(band) == 2 else (1,))
    for pole, step in poles:
        @pl.when(z == pole)
        def _():
            for i in range(2):
                for side in range(2):
                    fwd_copy(pole, step, i, side).wait_recv()

    def interpolate(t, carry):
        sources = [ext[where_ref[t * stencil + k]] for k in range(stencil)]
        block = weights[pl.ds(t * stencil, stencil)].reshape(stencil * cells, cells)
        value = jnp.dot(
            jnp.concatenate(sources, axis=1), block, preferred_element_type=jnp.float32
        )
        tangent_ref[t] = value.astype(jnp.bfloat16)
        return carry

    lax.fori_loop(0, targets, interpolate, 0, unroll=2)

    x_all(ax_copy, 0, ax_finish)
    here = at(place(0, HALO), tile)
    for d in range(2):
        @pl.when(there(-steps[d]))
        def _():
            for part in range(cols):
                az_copy(d, 1, part).wait_recv()
            spread[here, :] += near_in[d].astype(jnp.float32).reshape(tile * depth, cells)
    adjoint_ref[...] = spread[here, :].astype(jnp.bfloat16).reshape(tile, depth, cells)

    for band in range(-REACH, REACH + 1):
        x_all(x_copy, band, wait_send)
        x_all(ax_copy, band, wait_send)
    for pole, step in poles:
        for i in range(2):
            for side in range(2):
                @pl.when(z == pole)
                def _():
                    lend_copy(pole, step, i, side).wait_send()

                @pl.when(z == pole + step)
                def _():
                    fwd_copy(pole, step, i, side).wait_send()
    for d in range(2):
        @pl.when(there(steps[d]))
        def _():
            for part in range(2):
                z_copy(d, 0, part).wait_send()
            for part in range(cols):
                az_copy(d, 1, part).wait_send()

            @pl.when(there(-steps[d]))
            def _():
                for part in range(2):
                    z_copy(d, 1, part).wait_send()

        @pl.when(there(2 * steps[d]))
        def _():
            for part in range(cols):
                az_copy(d, 0, part).wait_send()


def on_device(perturbation, adjoint_forcing, source_rows, source_cols, cubic_weights):
    fields, levels, rows, cols, cells = perturbation.shape
    stencil = source_rows.shape[2]
    depth = fields * levels
    span = cols + 2 * HALO
    tile = rows * cols
    picks = tile * stencil
    places = BANDS * span * rows
    lat_count = lax.axis_size("lat")
    lon_count = lax.axis_size("lon")
    z = lax.axis_index("lat")
    x = lax.axis_index("lon")
    local_rows = source_rows - z * rows + REACH * rows
    local_cols = jnp.mod(source_cols - x * cols + HALO, cols * lon_count)
    where = ((local_rows // rows) * span + local_cols) * rows + local_rows % rows
    where = where.reshape(picks).astype(jnp.int32)
    onehot = jnp.arange(places, dtype=jnp.int32)[:, None] == jnp.tile(where, 2)[None, :]
    onehot = onehot.astype(jnp.bfloat16)
    own = perturbation.transpose(3, 2, 0, 1, 4).reshape(tile, depth, cells)
    forcing = adjoint_forcing.transpose(2, 3, 0, 1, 4).reshape(tile, depth, cells)
    weights = pltpu.with_memory_space_constraint(
        cubic_weights.reshape(picks, cells, cells), pltpu.HBM
    )

    vmem = pl.BlockSpec(memory_space=pltpu.VMEM)
    dma = pltpu.SemaphoreType.DMA
    bf16, f32 = jnp.bfloat16, jnp.float32
    tangent, adjoint = pl.pallas_call(
        functools.partial(exchange, (lat_count, lon_count, rows, cols, stencil)),
        name="exchange",
        out_shape=(
            jax.ShapeDtypeStruct((tile, depth, cells), bf16),
            jax.ShapeDtypeStruct((tile, depth, cells), bf16),
        ),
        in_specs=[
            pl.BlockSpec(memory_space=pltpu.SMEM),
            vmem,
            vmem,
            vmem,
            pl.BlockSpec(memory_space=pltpu.HBM),
        ],
        out_specs=(vmem, vmem),
        scratch_shapes=[
            pltpu.VMEM((places, depth, cells), bf16),
            pltpu.VMEM((picks, cells, cells), bf16),
            pltpu.VMEM((picks * depth, cells), f32),
            pltpu.VMEM((places * depth, cells), f32),
            pltpu.VMEM((BANDS, 2, 2, rows, depth, cells), bf16),
            pltpu.VMEM((BANDS, 2, 2, rows, depth, cells), bf16),
            pltpu.VMEM((2, 2, rows, depth, cells), bf16),
            pltpu.VMEM((2, cols, rows, depth, cells), bf16),
            pltpu.VMEM((2, cols, rows, depth, cells), bf16),
            pltpu.VMEM((2, cols, rows, depth, cells), bf16),
            pltpu.VMEM((2, cols, rows, depth, cells), bf16),
            dma,
            dma,
            dma((2, 2)),
            dma((2, 2)),
            dma((2, 2)),
            dma((2, 2)),
            dma((2, 2, 2)),
            dma((2, 2, 2)),
            dma((BANDS, 2, 2)),
            dma((BANDS, 2, 2)),
            dma((BANDS, 2, 2)),
            dma((BANDS, 2, 2)),
            dma((2, 2, cols)),
            dma((2, 2, cols)),
        ],
        compiler_params=pltpu.CompilerParams(
            collective_id=0, has_side_effects=True, vmem_limit_bytes=48 * 1024 * 1024
        ),
    )(where, own, forcing, onehot, weights)

    tangent_out = tangent.reshape(rows, cols, fields, levels, cells).transpose(2, 3, 0, 1, 4)
    adjoint_out = adjoint.reshape(cols, rows, fields, levels, cells).transpose(2, 3, 1, 0, 4)
    return (tangent_out, adjoint_out)


def solution(mesh):
    placed = (
        P("member", "lev", "lat", "lon", None),
        P("member", "lev", "lat", "lon", None),
        P("lat", "lon", None),
        P("lat", "lon", None),
        P("lat", "lon", None, None, None),
    )
    return jax.shard_map(
        on_device,
        mesh=mesh,
        in_specs=placed,
        out_specs=(P("member", "lev", "lat", "lon", None), P("member", "lev", "lat", "lon", None)),
        check_vma=False,
    )
```

profile of v0, /device:TPU:0, one launch (start us, length us, event | category | flops | bytes accessed | tf_op | source)
XLA Modules:
  0.0 42.4 jit_solution(7850376929190481094)
XLA Ops:
  0.6 0.7 %fusion.4 = s32[4,4,4]{2,1,0:T(4,128)S(1)} fusion(s32[4,4,4]{2,1,0:T(4,128)} %param.7, s32[4,4,4]{2,1,0:T(4,128)} %param.8, s32[]{:T(128)S(6)} %mul.15, s32[]{:T(128)S(6)} %mul.13), kind=kLoop, calls=%fused_computation.15 | loop fusion | flops 2432 | bytes 776 | tf_op jit(solution)/shard_map/add | solution.py:403
  1.4 0.1 reshape.24.where_ref
  1.5 0.1 eq.19
  1.6 1.0 %copy.7 = bf16[4,4,2,32,128]{4,3,2,1,0:T(8,128)(2,1)S(1)} copy(bf16[4,4,2,32,128]{4,0,1,3,2:T(4,128)(2,1)} %bitcast.18) | data formatting | bytes 524288 | tf_op jit(solution)/shard_map/transpose | solution.py:407
  2.6 1.0 %copy.8 = bf16[4,4,2,32,128]{4,3,2,1,0:T(8,128)(2,1)S(1)} copy(bf16[4,4,2,32,128]{4,1,0,3,2:T(4,128)(2,1)} %bitcast.19) | data formatting | bytes 524288 | tf_op jit(solution)/shard_map/transpose | solution.py:408
  3.6 36.9 %exchange.1 = (bf16[16,64,128]{2,1,0:T(8,128)(2,1)S(1)}, bf16[16,64,128]{2,1,0:T(8,128)(2,1)S(1)}) custom-call(s32[64]{0:T(128)S(1)} %reshape.24.where_ref, bf16[16,64,128]{2,1,0:T(8,128)(2,1)S(1)} %bitcast.13, bf16[16,64,128]{2,1,0:T(8,128)(2,1)S(1)} %bitcast.14, bf16[160,128]{1,0:T(8,128)(2,1)S(1)} %fusion.onehot_ref, bf16[64,128,128]{2,1,0:T(8,128)(2,1)} %bitcast.17), custom_call_target="tpu_custom_call" | custom-call | tf_op jit(solution)/shard_map/exchange/pallas_call | solution.py:416
  40.6 0.9 %copy.14 = bf16[4,4,2,32,128]{4,1,0,3,2:T(4,128)(2,1)} copy(bf16[4,4,2,32,128]{4,3,2,1,0:T(8,128)(2,1)S(1)} %bitcast.16) | data formatting | bytes 524288 | tf_op jit(solution)/shard_map/reshape | solution.py:463
  41.5 0.9 %copy.13 = bf16[4,4,2,32,128]{4,0,1,3,2:T(4,128)(2,1)} copy(bf16[4,4,2,32,128]{4,3,2,1,0:T(8,128)(2,1)S(1)} %bitcast.15) | data formatting | bytes 524288 | tf_op jit(solution)/shard_map/reshape | solution.py:464
  (2 shorter events, 0.0 us)
where the time goes:
time: 42.7 us; the launch traced here: 42.4 us
  Pallas kernels  36.9 us (86%)
  local copies, waits for them, and re-layouts  4.03 us (9%)
  other arithmetic  0.77 us (2%)
  between operations  0.67 us (2%)
    pallas_call x1, Pallas kernels, on_device(): pl.pallas_call(functools.partial(exchange, (lat_count, lon_count, rows, c...  36.9 us
    transpose x1, local copies, waits for them, and re-layouts, on_device(): own = perturbation.transpose(3, 2, 0, 1, 4).reshape(tile, depth, cells)  1.02 us
    transpose x1, local copies, waits for them, and re-layouts, on_device(): adjoint_forcing.transpose(2, 3, 0, 1, 4).reshape(tile, depth, cells)  1.02 us
    reshape x1, local copies, waits for them, and re-layouts, on_device(): tangent.reshape(rows, cols, fields, levels, cells).transpose(2, 3, 0, 1, 4)  0.91 us
    reshape x1, local copies, waits for them, and re-layouts, on_device(): adjoint.reshape(cols, rows, fields, levels, cells).transpose(2, 3, 1, 0, 4)  0.91 us

commit v1 on v0

v1 whole, which is shorter than its diff:
```python
import functools
import jax
import jax.numpy as jnp
from jax import lax
from jax.experimental import pallas as pl
from jax.experimental.pallas import tpu as pltpu
from jax.sharding import PartitionSpec as P

REACH = 2
HALO = 2
BANDS = 2 * REACH + 1
PAD = 8
STEPS = (1, -1)
MESH = pl.DeviceIdType.MESH
BF16, F32 = jnp.bfloat16, jnp.float32


def exchange(
    sizes,
    rows_ref, cols_ref, own_hbm, forcing_hbm, weights_hbm,
    tangent_ref, adjoint_ref,
    raw, forcing, weights, ext, picked, turned, spread, gather,
    ax_out, ax_in, far_out, far_in, near_out, near_in, lent,
    load_sem, zf_send, zf_recv, xf_send, xf_recv, ax_send, ax_recv, az_send, az_recv,
    fwd_send, fwd_recv, lend_send, lend_recv,
):
    lat_count, lon_count, rows, cols, stencil = sizes
    depth, tile, cells = raw.shape
    pair = 2 * rows
    sides = 1 if lon_count == 2 else 2
    group = tile + sides * tile
    places = BANDS * group
    picks = tile * stencil
    pitch = depth + PAD
    total_cols = cols * lon_count
    lat_rows = (2 * REACH + 1) * rows
    z = lax.axis_index("lat")
    x = lax.axis_index("lon")
    east = lax.rem(x + 1, lon_count)
    west = lax.rem(x + lon_count - 1, lon_count)
    out_side = (east, west)[:sides]
    back = (0,) if sides == 1 else (1, 0)
    last = lat_count - 1
    polar = (z == 0) | (z == last)
    inland = jnp.logical_not(polar)
    poles = ((0, 1), (last, -1))
    kinds = (0, 1)

    def there(offset):
        return (z + offset >= 0) & (z + offset < lat_count)

    def slot(band, kind, side=None):
        first = (band + REACH) * group + kind * pair
        if side is not None:
            first += tile * (1 + side)
        return pl.ds(first, pair)

    def when(condition, act):
        pl.when(condition)(act)

    def loads():
        return (
            pltpu.make_async_copy(own_hbm, raw, load_sem.at[0]),
            pltpu.make_async_copy(forcing_hbm, forcing, load_sem.at[1]),
            pltpu.make_async_copy(weights_hbm, weights, load_sem.at[2]),
        )

    barrier = pltpu.get_barrier_semaphore()
    for side in out_side:
        pl.semaphore_signal(barrier, inc=1, device_id={"lon": side}, device_id_type=MESH)
    for step in STEPS:
        @pl.when(there(step))
        def _():
            pl.semaphore_signal(barrier, inc=1, device_id={"lat": z + step}, device_id_type=MESH)
    for copy in loads():
        copy.start()

    def zf(d, hop, kind):
        band = -STEPS[d] * hop
        return pltpu.make_async_remote_copy(
            src_ref=ext.at[:, slot(band, kind), :],
            dst_ref=ext.at[:, slot(band - STEPS[d], kind), :],
            send_sem=zf_send.at[d, hop, kind],
            recv_sem=zf_recv.at[d, hop, kind],
            device_id={"lat": z + STEPS[d]},
            device_id_type=MESH,
        )

    def xf(band, kind, side):
        return pltpu.make_async_remote_copy(
            src_ref=ext.at[:, slot(band, kind), :],
            dst_ref=ext.at[:, slot(band, kind, back[side]), :],
            send_sem=xf_send.at[band + REACH, kind, side],
            recv_sem=xf_recv.at[band + REACH, kind, back[side]],
            device_id={"lon": out_side[side]},
            device_id_type=MESH,
        )

    def xf_in(band, kind, side):
        return pltpu.make_async_remote_copy(
            src_ref=ext.at[:, slot(band, kind), :],
            dst_ref=ext.at[:, slot(band, kind, side), :],
            send_sem=xf_send.at[band + REACH, kind, side],
            recv_sem=xf_recv.at[band + REACH, kind, side],
            device_id={"lon": out_side[side]},
            device_id_type=MESH,
        )

    def ax(band, kind, side, arrive=False):
        land = side if arrive else back[side]
        return pltpu.make_async_remote_copy(
            src_ref=ax_out.at[band + REACH, side, kind],
            dst_ref=ax_in.at[band + REACH, land, kind],
            send_sem=ax_send.at[band + REACH, kind, side],
            recv_sem=ax_recv.at[band + REACH, kind, land],
            device_id={"lon": out_side[side]},
            device_id_type=MESH,
        )

    def az(d, near, kind):
        return pltpu.make_async_remote_copy(
            src_ref=(near_out if near else far_out).at[d, kind],
            dst_ref=(near_in if near else far_in).at[d, kind],
            send_sem=az_send.at[d, near, kind],
            recv_sem=az_recv.at[d, near, kind],
            device_id={"lat": z + STEPS[d]},
            device_id_type=MESH,
        )

    def fwd(pole, step, i, side):
        return pltpu.make_async_remote_copy(
            src_ref=ext.at[:, slot(i * step, 0, side), :],
            dst_ref=ext.at[:, slot((i + 1) * step, 0, side), :],
            send_sem=fwd_send.at[i, side],
            recv_sem=fwd_recv.at[i, side],
            device_id={"lat": pole},
            device_id_type=MESH,
        )

    def lend(pole, step, i, side):
        return pltpu.make_async_remote_copy(
            src_ref=ax_out.at[(i + 1) * step + REACH, side, 0],
            dst_ref=lent.at[i, side],
            send_sem=lend_send.at[i, side],
            recv_sem=lend_recv.at[i, side],
            device_id={"lat": pole + step},
            device_id_type=MESH,
        )

    def x_start(make, band, kind):
        for side in range(sides):
            make(band, kind, side).start()

    span = tile * 8
    to = lax.broadcasted_iota(jnp.int32, (span, span), 0)
    come = lax.broadcasted_iota(jnp.int32, (span, span), 1)

    def column_of(place):
        position = (place % tile) // rows
        return jnp.where(position < 2, position * (cols - 1), position - 1)

    def shuffle(a, b):
        same = (a // tile == b // tile) & (b % tile == (a % rows) * cols + column_of(a))
        return jnp.where(same, 1.0, 0.0).astype(BF16)

    order = shuffle(to, come)
    own = pl.ds(REACH * group, tile)
    loads()[0].wait()
    for i in range(depth // 8):
        block = raw[pl.ds(i * 8, 8)].reshape(span, cells)
        block = jnp.dot(order, block, preferred_element_type=F32).astype(BF16)
        ext[pl.ds(i * 8, 8), own, :] = block.reshape(8, tile, cells)

    greeted = sides + jnp.where(there(1), 1, 0) + jnp.where(there(-1), 1, 0)
    pl.semaphore_wait(barrier, greeted)

    for kind in kinds:
        for d in range(2):
            when(there(STEPS[d]), lambda: zf(d, 0, kind).start())
        if kind == 0:
            x_start(xf, 0, 0)
        else:
            when(polar, lambda: x_start(xf, 0, 1))

    blank = jnp.zeros((depth, tile, cells), BF16)
    for band in range(-REACH, REACH + 1):
        @pl.when(jnp.logical_not(there(band)))
        def _():
            for part in range(group // tile):
                ext[:, pl.ds((band + REACH) * group + part * tile, tile), :] = blank

        @pl.when(there(band) & inland)
        def _():
            for side in range(sides):
                ext[:, slot(band, 1, side), :] = jnp.zeros((depth, pair, cells), BF16)

    lane = lax.broadcasted_iota(jnp.int32, (1, places), 1)
    within = lane % group
    half = within % tile
    position = HALO + jnp.where(half // rows < 2, (half // rows) * (cols - 1), half // rows - 1)
    area = within // tile
    position = position + jnp.where(area == 1, cols, jnp.where(area == 2, -cols, 0))
    position = (position + total_cols) % total_cols
    code = position * lat_rows + (lane // group) * rows + half % rows

    def select(t, carry):
        i, j = t // cols, t % cols
        for k in range(stencil):
            row = rows_ref[i, j, k] - z * rows + REACH * rows
            col = cols_ref[i, j, k] - x * cols + HALO
            col = col + jnp.where(col < 0, total_cols, 0)
            col = col - jnp.where(col >= total_cols, total_cols, 0)
            gather[pl.ds(t * stencil + k, 1), :] = jnp.where(
                code == col * lat_rows + row, 1.0, 0.0
            )
        return carry

    lax.fori_loop(0, tile, select, 0, unroll=2)
    chosen = gather[...]
    scatter = chosen.T.astype(BF16)

    loads()[1].wait()

    def turn(d, carry):
        turned[pl.ds(d, tile, stride=pitch), :] = forcing[d].astype(F32)
        return carry

    lax.fori_loop(0, depth, turn, 0, unroll=8)
    loads()[2].wait()

    def contribute(t, carry):
        block = weights[pl.ds(t * stencil, stencil)].reshape(stencil * cells, cells)
        here = turned[pl.ds(pl.multiple_of(t * pitch, 8), depth), :].astype(BF16)
        part = lax.dot_general(
            here, block, (((1,), (1,)), ((), ())), preferred_element_type=F32
        )
        for k in range(stencil):
            picked[pl.ds(t * stencil + k, depth, stride=picks + PAD), :] = part[
                :, k * cells : (k + 1) * cells
            ]
        return carry

    lax.fori_loop(0, tile, contribute, 0, unroll=2)

    def add_up(i, carry):
        pieces = []
        for e in range(2):
            first = pl.multiple_of((i * 2 + e) * (picks + PAD), 8)
            pieces.append(picked[pl.ds(first, picks), :].astype(BF16))
        summed = jnp.dot(
            scatter, jnp.concatenate(pieces, axis=1), preferred_element_type=F32
        )
        for e in range(2):
            d = i * 2 + e
            value = summed[:, e * cells : (e + 1) * cells]
            for band in range(BANDS):
                first = band * group
                spread[d, pl.ds(band * tile, tile), :] = value[first : first + tile]
                for side in range(sides):
                    first += tile
                    for kind in kinds:
                        ax_out[band, side, kind, d] = value[
                            first + kind * pair : first + (kind + 1) * pair
                        ].astype(BF16)
        return carry

    lax.fori_loop(0, depth // 2, add_up, 0, unroll=2)

    def total(band, kind):
        return spread.at[:, pl.ds((band + REACH) * tile + kind * pair, pair), :]

    def take(band, kind):
        for side in range(sides):
            ax(band, kind, side, True).wait_recv()
            total(band, kind)[...] += ax_in[band + REACH, side, kind].astype(F32)

    def send_far(d, kind):
        far_out[d, kind] = total(2 * STEPS[d], kind)[...].astype(BF16)
        az(d, 0, kind).start()

    def send_near(d, kind):
        @pl.when(there(-STEPS[d]))
        def _():
            az(d, 0, kind).wait_recv()
            total(STEPS[d], kind)[...] += far_in[d, kind].astype(F32)

        near_out[d, kind] = total(STEPS[d], kind)[...].astype(BF16)
        az(d, 1, kind).start()

    def borrow(pole, step, i):
        for side in range(sides):
            lend(pole, step, i, side).wait_recv()
            mine = ax_out.at[i * step + REACH, side, 0]
            mine[...] = (mine[...].astype(F32) + lent[i, side].astype(F32)).astype(BF16)
        x_start(ax, i * step, 0)

    for pole, step in poles:
        @pl.when(z == pole)
        def _():
            x_start(ax, 2 * step, 1)
            for side in range(sides):
                lend(pole, step, 1, side).start()
    for d in range(2):
        when(there(2 * STEPS[d]) & inland, lambda: x_start(ax, 2 * STEPS[d], 0))
    for pole, step in poles:
        when(z == pole, lambda: send_far(STEPS.index(step), 0))
    for d in range(2):
        @pl.when(there(-STEPS[d]))
        def _():
            zf(d, 0, 0).wait_recv()
            when(there(STEPS[d]), lambda: zf(d, 1, 0).start())
    for pole, step in poles:
        @pl.when(z == pole + step)
        def _():
            for side in range(sides):
                xf_in(0, 0, side).wait_recv()
            for side in range(sides):
                fwd(pole, step, 0, side).start()
            x_start(xf, step, 0)
            x_start(ax, -step, 0)
    inner = (z > 1) & (z < last - 1)

    @pl.when(inner)
    def _():
        for step in STEPS:
            x_start(ax, step, 0)
            x_start(xf, step, 0)

    for d in range(2):
        when(there(2 * STEPS[d]) & inland, lambda: send_far(d, 1))
    for d in range(2):
        @pl.when(there(-STEPS[d]))
        def _():
            zf(d, 0, 1).wait_recv()
            when(there(STEPS[d]), lambda: zf(d, 1, 1).start())
    for pole, step in poles:
        @pl.when(z == pole)
        def _():
            x_start(xf, step, 1)
            x_start(ax, step, 1)
            take(2 * step, 1)
            send_far(STEPS.index(step), 1)
            for side in range(sides):
                lend(pole, step, 0, side).start()
            send_near(STEPS.index(step), 0)
    for d in range(2):
        @pl.when(there(2 * STEPS[d]) & inland)
        def _():
            take(2 * STEPS[d], 0)
            send_far(d, 0)
    for pole, step in poles:
        @pl.when(z == pole + step)
        def _():
            borrow(pole, step, 1)
            x_start(xf, -step, 0)
            for side in range(sides):
                xf_in(step, 0, side).wait_recv()
            for side in range(sides):
                fwd(pole, step, 1, side).start()
    for d in range(2):
        @pl.when(there(-2 * STEPS[d]))
        def _():
            zf(d, 1, 0).wait_recv()
            when(inland, lambda: x_start(xf, -2 * STEPS[d], 0))
    for d in range(2):
        @pl.when(there(-2 * STEPS[d]))
        def _():
            zf(d, 1, 1).wait_recv()
            when(polar, lambda: x_start(xf, -2 * STEPS[d], 1))
    when(inner, lambda: x_start(ax, 0, 0))
    for pole, step in poles:
        @pl.when(z == pole)
        def _():
            x_start(ax, 0, 0)
            x_start(ax, 0, 1)
    for pole, step in poles:
        @pl.when(z == pole)
        def _():
            take(step, 1)
            send_near(STEPS.index(step), 1)

        @pl.when(z == pole + step)
        def _():
            send_near(STEPS.index(step), 1)
            take(-step, 0)
            send_near(STEPS.index(-step), 0)
            send_near(STEPS.index(-step), 1)
            take(step, 0)
            send_near(STEPS.index(step), 0)
            borrow(pole, step, 0)

    @pl.when(inner)
    def _():
        for d in range(2):
            send_near(d, 1)
        for d in range(2):
            take(STEPS[d], 0)
            send_near(d, 0)

    for pole, step in poles:
        @pl.when(z == pole)
        def _():
            for side in range(sides):
                for kind in kinds:
                    xf_in(0, kind, side).wait_recv()
                for i in range(2):
                    xf_in((i + 1) * step, 1, side).wait_recv()
                    fwd(pole, step, i, side).wait_recv()

        @pl.when(z == pole + step)
        def _():
            for side in range(sides):
                xf_in(-step, 0, side).wait_recv()

    @pl.when(inner)
    def _():
        for band in range(-1, 2):
            for side in range(sides):
                xf_in(band, 0, side).wait_recv()

    for d in range(2):
        @pl.when(there(2 * STEPS[d]) & inland)
        def _():
            for side in range(sides):
                xf_in(2 * STEPS[d], 0, side).wait_recv()

    chosen = gather[...].astype(BF16)

    def collect(i, carry):
        block = jnp.concatenate([ext[i * 2], ext[i * 2 + 1]], axis=1)
        value = jnp.dot(chosen, block, preferred_element_type=F32)
        for e in range(2):
            picked[pl.ds(i * 2 + e, picks, stride=pitch), :] = value[
                :, e * cells : (e + 1) * cells
            ]
        return carry

    lax.fori_loop(0, depth // 2, collect, 0, unroll=2)

    def interpolate(t, carry):
        sources = []
        for k in range(stencil):
            first = pl.multiple_of((t * stencil + k) * pitch, 8)
            sources.append(picked[pl.ds(first, depth), :].astype(BF16))
        block = weights[pl.ds(t * stencil, stencil)].reshape(stencil * cells, cells)
        value = jnp.dot(
            jnp.concatenate(sources, axis=1), block, preferred_element_type=F32
        )
        tangent_ref[t] = value.astype(BF16)
        return carry

    lax.fori_loop(0, tile, interpolate, 0, unroll=2)

    take(0, 0)
    when(polar, lambda: take(0, 1))
    for d in range(2):
        @pl.when(there(-STEPS[d]))
        def _():
            for kind in kinds:
                az(d, 1, kind).wait_recv()
                total(0, kind)[...] += near_in[d, kind].astype(F32)
    order = shuffle(come, to)
    for i in range(depth // 8):
        block = spread[pl.ds(i * 8, 8), pl.ds(REACH * tile, tile), :].astype(BF16)
        block = jnp.dot(order, block.reshape(span, cells), preferred_element_type=F32)
        adjoint_ref[pl.ds(i * 8, 8)] = block.astype(BF16).reshape(8, tile, cells)

    for d in range(2):
        @pl.when(there(STEPS[d]))
        def _():
            for kind in kinds:
                zf(d, 0, kind).wait_send()
                az(d, 1, kind).wait_send()

                @pl.when(there(-STEPS[d]))
                def _():
                    zf(d, 1, kind).wait_send()

                @pl.when(there(2 * STEPS[d]))
                def _():
                    az(d, 0, kind).wait_send()
    for side in range(sides):
        for make in (xf, ax):
            make(0, 0, side).wait_send()
            for band in range(-REACH, REACH + 1):
                if band != 0:
                    when(there(band) & inland, lambda: make(band, 0, side).wait_send())
                when(there(band) & polar, lambda: make(band, 1, side).wait_send())
        for pole, step in poles:
            for i in range(2):
                when(z == pole, lambda: lend(pole, step, i, side).wait_send())
                when(z == pole + step, lambda: fwd(pole, step, i, side).wait_send())


def on_device(perturbation, adjoint_forcing, source_rows, source_cols, cubic_weights):
    fields, levels, rows, cols, cells = perturbation.shape
    stencil = source_rows.shape[2]
    depth = fields * levels
    tile = rows * cols
    picks = tile * stencil
    lat_count = lax.axis_size("lat")
    lon_count = lax.axis_size("lon")
    assert cols == 2 * HALO and rows >= 4 and lat_count >= 4 and lon_count >= 2
    sides = 1 if lon_count == 2 else 2
    places = BANDS * tile * (1 + sides)
    half = (depth, 2 * rows, cells)
    own = perturbation.reshape(depth, tile, cells)
    forcing = adjoint_forcing.reshape(depth, tile, cells)
    weights = cubic_weights.reshape(picks, cells, cells)

    vmem = pl.BlockSpec(memory_space=pltpu.VMEM)
    hbm = pl.BlockSpec(memory_space=pltpu.HBM)
    smem = pl.BlockSpec(memory_space=pltpu.SMEM)
    dma = pltpu.SemaphoreType.DMA
    tangent, adjoint = pl.pallas_call(
        functools.partial(exchange, (lat_count, lon_count, rows, cols, stencil)),
        name="exchange",
        out_shape=(
            jax.ShapeDtypeStruct((tile, depth, cells), BF16),
            jax.ShapeDtypeStruct((depth, tile, cells), BF16),
        ),
        in_specs=[smem, smem, hbm, hbm, hbm],
        out_specs=(vmem, vmem),
        scratch_shapes=[
            pltpu.VMEM((depth, tile, cells), BF16),
            pltpu.VMEM((depth, tile, cells), BF16),
            pltpu.VMEM((picks, cells, cells), BF16),
            pltpu.VMEM((depth, places, cells), BF16),
            pltpu.VMEM((max(picks, depth) * (max(picks, depth) + PAD), cells), F32),
            pltpu.VMEM((tile * (depth + PAD), cells), F32),
            pltpu.VMEM((depth, BANDS * tile, cells), F32),
            pltpu.VMEM((picks, places), F32),
            pltpu.VMEM((BANDS, sides, 2) + half, BF16),
            pltpu.VMEM((BANDS, sides, 2) + half, BF16),
            pltpu.VMEM((2, 2) + half, BF16),
            pltpu.VMEM((2, 2) + half, BF16),
            pltpu.VMEM((2, 2) + half, BF16),
            pltpu.VMEM((2, 2) + half, BF16),
            pltpu.VMEM((2, sides) + half, BF16),
            dma((3,)),
            dma((2, 2, 2)),
            dma((2, 2, 2)),
            dma((BANDS, 2, sides)),
            dma((BANDS, 2, sides)),
            dma((BANDS, 2, sides)),
            dma((BANDS, 2, sides)),
            dma((2, 2, 2)),
            dma((2, 2, 2)),
            dma((2, sides)),
            dma((2, sides)),
            dma((2, sides)),
            dma((2, sides)),
        ],
        compiler_params=pltpu.CompilerParams(
            collective_id=0, has_side_effects=True, vmem_limit_bytes=56 * 1024 * 1024
        ),
    )(source_rows, source_cols, own, forcing, weights)

    tangent_out = tangent.reshape(rows, cols, fields, levels, cells).transpose(2, 3, 0, 1, 4)
    adjoint_out = adjoint.reshape(fields, levels, rows, cols, cells)
    return (tangent_out, adjoint_out)


def solution(mesh):
    placed = (
        P("member", "lev", "lat", "lon", None),
        P("member", "lev", "lat", "lon", None),
        P("lat", "lon", None),
        P("lat", "lon", None),
        P("lat", "lon", None, None, None),
    )
    return jax.shard_map(
        on_device,
        mesh=mesh,
        in_specs=placed,
        out_specs=(P("member", "lev", "lat", "lon", None), P("member", "lev", "lat", "lon", None)),
        check_vma=False,
    )
```

time: 42.7 us -> 38.5 us (0.902)
  the two profiles are of different devices: /device:TPU:0 before, /device:TPU:12 now
where the time goes in v1:
time: 38.5 us; the launch traced here: 38.2 us
  Pallas kernels  33.9 us (88%)
  local copies, waits for them, and re-layouts  3.6 us (9%)
  between operations  0.64 us (2%)
    pallas_call x1, Pallas kernels, on_device(): pl.pallas_call(functools.partial(exchange, (lat_count, lon_count, rows, c...  33.9 us
    reshape x1, local copies, waits for them, and re-layouts, on_device(): tangent.reshape(rows, cols, fields, levels, cells).transpose(2, 3, 0, 1, 4)  1.86 us
    unnamed x1, local copies, waits for them, and re-layouts  1.74 us

profile of v1, /device:TPU:12, one launch (start us, length us, event | category | flops | bytes accessed | tf_op | source)
XLA Modules:
  0.0 38.2 jit_solution(15680866036425605846)
XLA Ops:
  0.6 33.9 %exchange.1 = (bf16[16,64,128]{2,1,0:T(8,128)(2,1)}, bf16[64,16,128]{2,1,0:T(8,128)(2,1)}) custom-call(s32[4,4,4]{2,1,0:T(4,128)} %rows_ref.1, s32[4,4,4]{2,1,0:T(4,128)} %cols_ref.1, bf16[64,16,128]{2,1,0:T(8,128)(2,1)} %bitcast.9, bf16[64,16,128]{2,1,0:T(8,128)(2,1)} %bitcast.10, bf16[64,128,128]{2,1,0:T(8,128)(2,1)} %bitcast.8), custom_call_target="tpu_custom_call" | custom-call | tf_op jit(solution)/shard_map/exchange/pallas_call | solution.py:515
  34.6 1.9 %copy.9 = bf16[4,4,2,32,128]{4,1,0,3,2:T(4,128)(2,1)} copy(bf16[4,4,2,32,128]{4,3,2,1,0:T(8,128)(2,1)} %bitcast.13) | data formatting | bytes 524288 | tf_op jit(solution)/shard_map/reshape | solution.py:559
  36.4 1.7 %copy.11 = bf16[2,32,4,4,128]{4,3,2,1,0:T(4,128)(2,1)} copy(bf16[2,32,4,4,128]{4,3,2,1,0:T(4,128)(2,1)} %bitcast.12) | data formatting | bytes 524288

commit v2 on v1

--- a/solution.py
+++ b/solution.py
@@ -17,9 +17,9 @@
 
 def exchange(
     sizes,
-    rows_ref, cols_ref, own_hbm, forcing_hbm, weights_hbm,
+    rows_hbm, cols_hbm, own_hbm, forcing_hbm, weights_hbm,
     tangent_ref, adjoint_ref,
-    raw, forcing, weights, ext, picked, turned, spread, gather,
+    rows_ref, cols_ref, raw, forcing, weights, ext, picked, turned, spread, gather,
     ax_out, ax_in, far_out, far_in, near_out, near_in, lent,
     load_sem, zf_send, zf_recv, xf_send, xf_recv, ax_send, ax_recv, az_send, az_recv,
     fwd_send, fwd_recv, lend_send, lend_recv,
@@ -63,6 +63,8 @@
             pltpu.make_async_copy(own_hbm, raw, load_sem.at[0]),
             pltpu.make_async_copy(forcing_hbm, forcing, load_sem.at[1]),
             pltpu.make_async_copy(weights_hbm, weights, load_sem.at[2]),
+            pltpu.make_async_copy(rows_hbm, rows_ref, load_sem.at[3]),
+            pltpu.make_async_copy(cols_hbm, cols_ref, load_sem.at[4]),
         )
 
     barrier = pltpu.get_barrier_semaphore()
@@ -202,6 +204,9 @@
     position = position + jnp.where(area == 1, cols, jnp.where(area == 2, -cols, 0))
     position = (position + total_cols) % total_cols
     code = position * lat_rows + (lane // group) * rows + half % rows
+
+    for copy in loads()[3:]:
+        copy.wait()
 
     def select(t, carry):
         i, j = t // cols, t % cols
@@ -215,7 +220,7 @@
             )
         return carry
 
-    lax.fori_loop(0, tile, select, 0, unroll=2)
+    lax.fori_loop(0, tile, select, 0, unroll=8)
     chosen = gather[...]
     scatter = chosen.T.astype(BF16)
 
@@ -240,7 +245,7 @@
             ]
         return carry
 
-    lax.fori_loop(0, tile, contribute, 0, unroll=2)
+    lax.fori_loop(0, tile, contribute, 0, unroll=8)
 
     def add_up(i, carry):
         pieces = []
@@ -264,7 +269,7 @@
                         ].astype(BF16)
         return carry
 
-    lax.fori_loop(0, depth // 2, add_up, 0, unroll=2)
+    lax.fori_loop(0, depth // 2, add_up, 0, unroll=8)
 
     def total(band, kind):
         return spread.at[:, pl.ds((band + REACH) * tile + kind * pair, pair), :]
@@ -435,7 +440,7 @@
             ]
         return carry
 
-    lax.fori_loop(0, depth // 2, collect, 0, unroll=2)
+    lax.fori_loop(0, depth // 2, collect, 0, unroll=8)
 
     def interpolate(t, carry):
         sources = []
@@ -449,7 +454,7 @@
         tangent_ref[t] = value.astype(BF16)
         return carry
 
-    lax.fori_loop(0, tile, interpolate, 0, unroll=2)
+    lax.fori_loop(0, tile, interpolate, 0, unroll=8)
 
     take(0, 0)
     when(polar, lambda: take(0, 1))
@@ -504,13 +509,18 @@
     sides = 1 if lon_count == 2 else 2
     places = BANDS * tile * (1 + sides)
     half = (depth, 2 * rows, cells)
-    own = perturbation.reshape(depth, tile, cells)
-    forcing = adjoint_forcing.reshape(depth, tile, cells)
-    weights = cubic_weights.reshape(picks, cells, cells)
+    indices = [pltpu.with_memory_space_constraint(a, pltpu.HBM) for a in (source_rows, source_cols)]
+    own, forcing, weights = (
+        pltpu.with_memory_space_constraint(a, pltpu.HBM)
+        for a in (
+            perturbation.reshape(depth, tile, cells),
+            adjoint_forcing.reshape(depth, tile, cells),
+            cubic_weights.reshape(picks, cells, cells),
+        )
+    )
 
     vmem = pl.BlockSpec(memory_space=pltpu.VMEM)
     hbm = pl.BlockSpec(memory_space=pltpu.HBM)
-    smem = pl.BlockSpec(memory_space=pltpu.SMEM)
     dma = pltpu.SemaphoreType.DMA
     tangent, adjoint = pl.pallas_call(
         functools.partial(exchange, (lat_count, lon_count, rows, cols, stencil)),
@@ -519,9 +529,11 @@
             jax.ShapeDtypeStruct((tile, depth, cells), BF16),
             jax.ShapeDtypeStruct((depth, tile, cells), BF16),
         ),
-        in_specs=[smem, smem, hbm, hbm, hbm],
+        in_specs=[hbm] * 5,
         out_specs=(vmem, vmem),
         scratch_shapes=[
+            pltpu.SMEM(source_rows.shape, jnp.int32),
+            pltpu.SMEM(source_cols.shape, jnp.int32),
             pltpu.VMEM((depth, tile, cells), BF16),
             pltpu.VMEM((depth, tile, cells), BF16),
             pltpu.VMEM((picks, cells, cells), BF16),
@@ -537,7 +549,7 @@
             pltpu.VMEM((2, 2) + half, BF16),
             pltpu.VMEM((2, 2) + half, BF16),
             pltpu.VMEM((2, sides) + half, BF16),
-            dma((3,)),
+            dma((5,)),
             dma((2, 2, 2)),
             dma((2, 2, 2)),
             dma((BANDS, 2, sides)),
@@ -552,9 +564,9 @@
             dma((2, sides)),
         ],
         compiler_params=pltpu.CompilerParams(
-            collective_id=0, has_side_effects=True, vmem_limit_bytes=56 * 1024 * 1024
+            collective_id=0, has_side_effects=True, vmem_limit_bytes=24 * 1024 * 1024
         ),
-    )(source_rows, source_cols, own, forcing, weights)
+    )(*indices, own, forcing, weights)
 
     tangent_out = tangent.reshape(rows, cols, fields, levels, cells).transpose(2, 3, 0, 1, 4)
     adjoint_out = adjoint.reshape(fields, levels, rows, cols, cells)

time: 38.5 us -> 32.7 us (0.85)
  the two profiles are of different devices: /device:TPU:12 before, /device:TPU:0 now
where the time goes in v2:
time: 32.7 us; the launch traced here: 32.6 us
  Pallas kernels  30.3 us (93%)
  local copies, waits for them, and re-layouts  1.61 us (5%)
  between operations  0.64 us (2%)
    pallas_call x1, Pallas kernels, on_device(): pl.pallas_call(functools.partial(exchange, (lat_count, lon_count, rows, c...  30.3 us
    reshape x1, local copies, waits for them, and re-layouts, on_device(): tangent.reshape(rows, cols, fields, levels, cells).transpose(2, 3, 0, 1, 4)  0.91 us
    unnamed x1, local copies, waits for them, and re-layouts  0.7 us

profile of v2, /device:TPU:0, one launch (start us, length us, event | category | flops | bytes accessed | tf_op | source)
XLA Modules:
  0.0 32.6 jit_solution(3866124029548480590)
XLA Ops:
  0.6 30.3 %exchange.1 = (bf16[16,64,128]{2,1,0:T(8,128)(2,1)S(1)}, bf16[64,16,128]{2,1,0:T(8,128)(2,1)S(1)}) custom-call(s32[4,4,4]{2,1,0:T(4,128)} %rows_hbm.1, s32[4,4,4]{2,1,0:T(4,128)} %cols_hbm.1, bf16[64,16,128]{2,1,0:T(8,128)(2,1)} %bitcast.11, bf16[64,16,128]{2,1,0:T(8,128)(2,1)} %bitcast.12, bf16[64,128,128]{2,1,0:T(8,128)(2,1)} %bitcast.10), custom_call_target="tpu_custom_call" | custom-call | tf_op jit(solution)/shard_map/exchange/pallas_call | solution.py:525
  30.9 0.9 %copy.9 = bf16[4,4,2,32,128]{4,1,0,3,2:T(4,128)(2,1)} copy(bf16[4,4,2,32,128]{4,3,2,1,0:T(8,128)(2,1)S(1)} %bitcast.9) | data formatting | bytes 524288 | tf_op jit(solution)/shard_map/reshape | solution.py:571
  31.9 0.7 %copy.11 = bf16[2,32,4,4,128]{4,3,2,1,0:T(4,128)(2,1)} copy(bf16[2,32,4,4,128]{4,3,2,1,0:T(4,128)(2,1)S(1)} %bitcast.8) | data formatting | bytes 524288
